TPU v7x, 128 devices: a whole 4x4x4 slice. The times are simulated.
128 devices in a mesh: dp: 8 (over x, y_hi), expert: 16 (over z, y_lo, core).
Axes of the slice: x: 4, y: 4 (y_hi: 2, y_lo: 2; y = y_hi * 2 + y_lo), z: 4, core: 2. Of those that a mesh axis runs over, the one named last changes fastest.
Arguments:
- tokens: bfloat16 [16384, 4096], P(('dp', 'expert')), may hold values from -6 to 6
- cotangent: bfloat16 [16384, 4096], P(('dp', 'expert')), may hold values from -3 to 3
- expert_ids: int32 [16384, 8, 2], P(('dp', 'expert')), may hold values from 0 to 31, as said below
- slot_ids: int32 [16384, 8, 2], P(('dp', 'expert')), may hold values from 0 to 63, as said below
- route_probs: bfloat16 [16384, 8, 2], P(('dp', 'expert')), may hold values from 0.099609375 to 1
- weights_in: bfloat16 [32, 2, 1792, 512], P('expert', None, 'dp'), may hold values from -0.25 to 0.25
- weights_out: bfloat16 [32, 1792, 512], P('expert', 'dp'), may hold values from -0.125 to 0.125
Outputs:
- grad_tokens: bfloat16 [16384, 4096], P(('dp', 'expert'))
- grad_probs: float32 [16384, 8, 2], P(('dp', 'expert'))
- grad_in: bfloat16 [32, 2, 1792, 512], P('expert', None, 'dp')
- grad_out: bfloat16 [32, 1792, 512], P('expert', 'dp')
Inputs may be any that keep to these rules, and one draw needn't show every extreme that they name: `expert_ids`: each sub-token names 2 different experts. On each device the experts fall into two sets of 16, and the two ids of a sub-token come one from each set. Every expert is named by exactly 64 sub-tokens of every device. `slot_ids`: for each device and expert, the sub-tokens of that device that name the expert carry distinct slot numbers at the matching position.
All inputs are finite; a program needn't handle non-finite values.
Results may differ from a plain program's by a relative error of at most 0.012.
Values may be sent and summed in bfloat16 or wider, within the bound.
No kernel may reach another device: no remote copies, remote signals or barrier semaphores. Data moves between devices by JAX's collectives and lax.ppermute only.
A program may use at most 192 MiB of HBM per device.

v0:
```python
import math
import jax
import jax.numpy as jnp
from jax import lax
from jax.sharding import PartitionSpec as P

H = 8
DS = 512


def side_by_side(arrays, axis, split_dim, concat_dim, along):
    widths = [math.prod(a.shape[along:]) for a in arrays]
    both = jnp.concatenate(
        [a.reshape(*a.shape[:along], w) for a, w in zip(arrays, widths)], axis=along
    )
    filled = lax.all_to_all(both, axis, split_axis=split_dim, concat_axis=concat_dim, tiled=True)
    tiles = jnp.split(filled, [sum(widths[:k]) for k in range(1, len(widths))], axis=along)
    return tuple(
        (b.reshape(*filled.shape[:along], *a.shape[along:]) for a, b in zip(arrays, tiles))
    )


def rows_first(arrays, axis, dims):
    turned = [jnp.moveaxis(a, dim, 0) for a, dim in zip(arrays, dims)]
    widths = [t[0].size for t in turned]
    both = jnp.concatenate([t.reshape(-1, w) for t, w in zip(turned, widths)], axis=1)
    filled = lax.all_gather(both, axis, axis=0, tiled=True)
    tiles = jnp.split(filled, [sum(widths[:k]) for k in range(1, len(widths))], axis=1)
    return tuple(
        (
            jnp.moveaxis(b.reshape(-1, *t.shape[1:]), 0, dim)
            for b, t, dim in zip(tiles, turned, dims)
        )
    )


def contract_last(former, latter):
    return lax.dot_general(
        former, latter, (((1,), (1,)), ((), ())), preferred_element_type=jnp.float32
    )


def expert_backward(inputs, cotangent, weighting, gate_up, down_proj):
    gate_pre = contract_last(inputs, gate_up[0])
    up_pre = contract_last(inputs, gate_up[1])
    sigmoids = jax.nn.sigmoid(gate_pre)
    activated = gate_pre * sigmoids
    hidden = (activated * up_pre).astype(jnp.bfloat16)
    output = jnp.dot(hidden, down_proj, preferred_element_type=jnp.float32)
    router_grad = jnp.sum(output * cotangent.astype(jnp.float32), axis=1).astype(jnp.bfloat16)
    scaled = (weighting.astype(jnp.float32)[:, None] * cotangent.astype(jnp.float32)).astype(
        jnp.bfloat16
    )
    dhidden = contract_last(scaled, down_proj)
    gate_grad = (dhidden * up_pre * sigmoids * (1.0 + gate_pre * (1.0 - sigmoids))).astype(
        jnp.bfloat16
    )
    up_grad = (dhidden * activated).astype(jnp.bfloat16)
    input_grad = jnp.dot(gate_grad, gate_up[0], preferred_element_type=jnp.float32)
    input_grad = (
        input_grad + jnp.dot(up_grad, gate_up[1], preferred_element_type=jnp.float32)
    ).astype(jnp.bfloat16)
    return (input_grad, router_grad, gate_grad, up_grad, hidden, scaled)


def reduce_grads(inputs, gate_grad, up_grad, hidden, scaled):
    gate_term = jnp.einsum("rf,rd->fd", gate_grad, inputs, preferred_element_type=jnp.float32)
    up_term = jnp.einsum("rf,rd->fd", up_grad, inputs, preferred_element_type=jnp.float32)
    summed = lax.psum_scatter(
        jnp.concatenate(
            [
                jnp.stack([gate_term, up_term], axis=1),
                jnp.einsum("rf,rd->fd", hidden, scaled, preferred_element_type=jnp.float32)[
                    :, None, :
                ],
            ],
            axis=1,
        ).astype(jnp.bfloat16),
        "dp",
        scatter_dimension=0,
        tiled=True,
    ).astype(jnp.float32)
    pair_sum = summed[:, :2]
    down_sum = summed[:, 2]
    return (jnp.transpose(pair_sum, (1, 0, 2)).astype(jnp.bfloat16), down_sum.astype(jnp.bfloat16))


def body(tokens, cotangent, expert_ids, slot_ids, route_probs, weights_in, weights_out):
    peers = lax.axis_size("expert")
    local_count = weights_in.shape[0]
    token_count = tokens.shape[0]
    sub_count = token_count * H
    capacity = sub_count * 2 // (local_count * peers)
    buffer_rows = local_count * peers * capacity
    chosen = expert_ids.reshape(sub_count, 2)
    placed = (
        chosen % local_count * (peers * capacity)
        + chosen // local_count * capacity
        + slot_ids.reshape(sub_count, 2)
    )
    flat_place = placed.reshape(-1)

    def spread(values):
        doubled = jnp.broadcast_to(values[:, None, :], (sub_count, 2, DS)).reshape(
            2 * sub_count, DS
        )
        filled = jnp.zeros((buffer_rows, DS), jnp.bfloat16).at[flat_place].set(doubled)
        return filled.reshape(local_count, peers, capacity, DS)

    input_buffer = spread(tokens.reshape(sub_count, DS))
    cotangent_buffer = spread(cotangent.reshape(sub_count, DS))
    prob_buffer = (
        jnp.zeros((buffer_rows,), jnp.bfloat16).at[flat_place].set(route_probs.reshape(-1))
    )
    prob_buffer = prob_buffer.reshape(local_count, peers, capacity)
    arrived_in = lax.all_to_all(input_buffer, "expert", split_axis=1, concat_axis=1, tiled=True)
    arrived_cot, arrived_prob = side_by_side((cotangent_buffer, prob_buffer), "expert", 1, 1, 3)
    input_grads = []
    router_grads = []
    grads_pair = []
    grads_down = []
    for expert_pos in range(local_count):
        single_in, single_out = rows_first(
            (weights_in[expert_pos : expert_pos + 1], weights_out[expert_pos : expert_pos + 1]),
            "dp",
            (2, 1),
        )
        gate_up = single_in[0]
        down_proj = single_out[0]
        rows_in = arrived_in[expert_pos].reshape(peers * capacity, DS)
        rows_cot = arrived_cot[expert_pos].reshape(peers * capacity, DS)
        rows_prob = arrived_prob[expert_pos].reshape(peers * capacity)
        input_grad, router_grad, gate_grad, up_grad, hidden, scaled = expert_backward(
            rows_in, rows_cot, rows_prob, gate_up, down_proj
        )
        pair_part, down_part = reduce_grads(rows_in, gate_grad, up_grad, hidden, scaled)
        input_grads.append(input_grad)
        router_grads.append(router_grad)
        grads_pair.append(pair_part)
        grads_down.append(down_part)
    stacked_inputs = jnp.stack(input_grads).reshape(local_count, peers, capacity, DS)
    stacked_router = jnp.stack(router_grads).reshape(local_count, peers, capacity)
    returned, returned_router = side_by_side((stacked_inputs, stacked_router), "expert", 1, 1, 3)
    back_rows = (
        returned.reshape(buffer_rows, DS)[flat_place].reshape(sub_count, 2, DS).astype(jnp.float32)
    )
    grad_tokens = jnp.sum(back_rows, axis=1).astype(jnp.bfloat16).reshape(token_count, H * DS)
    grad_probs = (
        returned_router.reshape(buffer_rows)[flat_place]
        .reshape(token_count, H, 2)
        .astype(jnp.float32)
    )
    return (grad_tokens, grad_probs, jnp.stack(grads_pair), jnp.stack(grads_down))


def solution(mesh):
    return jax.shard_map(
        body,
        mesh=mesh,
        in_specs=(
            P(("dp", "expert"), None),
            P(("dp", "expert"), None),
            P(("dp", "expert"), None, None),
            P(("dp", "expert"), None, None),
            P(("dp", "expert"), None, None),
            P("expert", None, "dp", None),
            P("expert", "dp", None),
        ),
        out_specs=(
            P(("dp", "expert"), None),
            P(("dp", "expert"), None, None),
            P("expert", None, "dp", None),
            P("expert", "dp", None),
        ),
        check_vma=False,
    )
```

profile of v0, /device:TPU:0, one launch (start us, length us, event | category | flops | bytes accessed | tf_op | source)
XLA Modules:
  0.0 402.9 jit_solution(530225747279303801)
XLA Ops:
  15.4 2.2 reshape.320
  17.7 10.6 %scatter_custom_fusion.2 = bf16[2048,512]{1,0:T(8,128)(2,1)S(1)} fusion(s32[2048]{0:T(1024)S(1)} %bitcast.149, bf16[2048,512]{1,0:T(8,128)(2,1)} %reshape.320, bf16[]{:T(256)} %constant.31.clone.1), kind=kCustom, calls=%fused_computation.59 | custom fusion | bytes 2097664 | tf_op jit(solution)/shard_map/scatter | solution.py:107
  29.8 6.8 %all-to-all-start.1 = ((bf16[2,16,64,512]{3,2,0,1:T(8,128)(2,1)}), bf16[2,16,64,512]{3,2,0,1:T(8,128)(2,1)S(1)}, u32[]{:S(2)}, u32[]{:S(2)}) async-start(bf16[2,16,64,512]{3,2,0,1:T(8,128)(2,1)} %copy.47), calls=%async_computation.1 | async-start | bytes 4194304 | tf_op jit(solution)/shard_map/all_to_all | solution.py:116
  37.1 14.6 %scatter_custom_fusion.1 = bf16[2048]{0:T(1024)(128)(2,1)S(1)} fusion(s32[2048]{0:T(1024)S(1)} %bitcast.150, bf16[2048]{0:T(1024)(128)(2,1)S(1)} %reshape.312, bf16[]{:T(256)} %constant.31.clone.1), kind=kCustom, calls=%fused_computation.88 | custom fusion | bytes 4098 | tf_op jit(solution)/shard_map/scatter | solution.py:113
  55.1 2.4 broadcast_in_dim.33
  57.5 4.2 %reshape.304 = bf16[2048,512]{1,0:T(8,128)(2,1)} reshape(bf16[1024,2,512]{2,1,0:T(2,128)(2,1)} %broadcast_in_dim.33) | data formatting | bytes 4194304 | tf_op jit(solution)/shard_map/reshape | solution.py:104
  61.7 11.5 %scatter_custom_fusion = bf16[2048,512]{1,0:T(8,128)(2,1)} fusion(s32[2048]{0:T(1024)S(1)} %bitcast.151, bf16[2048,512]{1,0:T(8,128)(2,1)} %reshape.304, bf16[]{:T(256)} %constant.31.clone.1), kind=kCustom, calls=%fused_computation.61 | custom fusion | bytes 2097664 | tf_op jit(solution)/shard_map/scatter | solution.py:107
  73.2 2.0 pad_maximum_fusion.2
  78.3 5.8 %all-to-all-start = ((bf16[2,16,64,513]{3,2,0,1:T(8,128)(2,1)}), bf16[2,16,64,513]{3,2,0,1:T(8,128)(2,1)S(1)}, u32[]{:S(2)}, u32[]{:S(2)}) async-start(bf16[2,16,64,513]{3,2,0,1:T(8,128)(2,1)} %copy.44), calls=%async_computation | async-start | bytes 5242880 | tf_op jit(solution)/shard_map/all_to_all | solution.py:16
  84.2 3.1 fusion.32
  87.3 35.7 %all-to-all-done = bf16[2,16,64,513]{3,2,0,1:T(8,128)(2,1)S(1)} async-done(((bf16[2,16,64,513]{3,2,0,1:T(8,128)(2,1)}), bf16[2,16,64,513]{3,2,0,1:T(8,128)(2,1)S(1)}, u32[]{:S(2)}, u32[]{:S(2)}) %all-to-all-start) | async-done | bytes 2101280 | tf_op jit(solution)/shard_map/all_to_all | solution.py:16
  125.9 4.2 %split.29 = bf16[1792,1024]{1,0:T(8,128)(2,1)} slice(bf16[1792,1536]{1,0:T(8,128)(2,1)} %all-gather.5.cloned.1.call-done), slice={[0:1792], [0:1024]} | slice | bytes 7340032 | tf_op jit(solution)/shard_map/split | solution.py:28
  130.1 7.6 %reshape.275 = bf16[1792,1,2,512]{3,2,0,1:T(2,128)(2,1)} reshape(bf16[1792,1024]{1,0:T(8,128)(2,1)} %split.29) | data formatting | bytes 7340032 | tf_op jit(solution)/shard_map/reshape | solution.py:31
  137.8 2.7 copy.66
  140.5 2.1 fusion.13
  142.6 6.6 %fusion.17 = f32[1024,1792]{1,0:T(8,128)} fusion(bf16[1024,512]{1,0:T(8,128)(2,1)S(1)} %multiply_convert_fusion.6, bf16[1792,1536]{1,0:T(8,128)(2,1)} %all-gather.5.cloned.1.call-done), kind=kOutput, calls=%fused_computation.52 | convolution fusion | flops 1879048192 | bytes 10223616 | tf_op jit(solution)/shard_map/dot_general | solution.py:38
  149.3 9.4 %multiply_convert_fusion.3 = (bf16[1024,1792]{1,0:T(8,128)(2,1)S(1)}, bf16[1024,1792]{1,0:T(8,128)(2,1)}, bf16[1024,1792]{1,0:T(8,128)(2,1)}) fusion(f32[1024,1792]{1,0:T(8,128)} %fusion.17, f32[1024,1792]{1,0:T(8,128)S(1)} %fusion.13, bf16[1024,512]{1,0:T(8,128)(2,1)S(1)} %bitcast.146, bf16[1,2,1792,512]{3,2,1,0:T(8,128)(2,1)S(1)} %bitcast.128), kind=kOutput, calls=%fused_computation.8 | convolution fusion | flops 1906573312 | bytes 28573696 | tf_op jit(solution)/shard_map/dot_general | solution.py:38
  158.7 5.5 %fusion.7 = bf16[1792,1,512]{2,0,1:T(8,128)(2,1)S(1)} fusion(bf16[1024,1792]{1,0:T(8,128)(2,1)} %get-tuple-element.22, bf16[1024,512]{1,0:T(8,128)(2,1)S(1)} %multiply_convert_fusion.6), kind=kOutput, calls=%fused_computation.30 | convolution fusion | flops 1879965696 | bytes 6553600 | tf_op jit(solution)/shard_map/rf,rd->fd/dot_general | solution.py:73
  164.3 2.1 fusion.6
  166.4 2.1 fusion.5
  168.6 3.0 pad_maximum_fusion.1
  173.1 21.6 %all-gather.3.cloned.1.call-done = bf16[1792,1536]{1,0:T(8,128)(2,1)} async-done(((bf16[224,1536]{1,0:T(8,128)(2,1)}), bf16[1792,1536]{1,0:T(8,128)(2,1)}) %all-gather.3.cloned.1.call-update) | async-done | bytes 5505040 | tf_op jit(solution)/shard_map/all_gather | solution.py:27
  194.7 4.2 %split.27 = bf16[1792,1024]{1,0:T(8,128)(2,1)} slice(bf16[1792,1536]{1,0:T(8,128)(2,1)} %all-gather.3.cloned.1.call-done), slice={[0:1792], [0:1024]} | slice | bytes 7340032 | tf_op jit(solution)/shard_map/split | solution.py:28
  198.9 7.3 %reshape.273 = bf16[1792,1,2,512]{3,2,0,1:T(2,128)(2,1)} reshape(bf16[1792,1024]{1,0:T(8,128)(2,1)} %split.27) | data formatting | bytes 7340032 | tf_op jit(solution)/shard_map/reshape | solution.py:31
  206.2 2.7 copy.67
  208.9 2.1 fusion.9
  211.0 6.5 %fusion.20 = f32[1024,1792]{1,0:T(8,128)} fusion(bf16[1024,512]{1,0:T(8,128)(2,1)S(1)} %multiply_convert_fusion.7, bf16[1792,1536]{1,0:T(8,128)(2,1)} %all-gather.3.cloned.1.call-done), kind=kOutput, calls=%fused_computation.55 | convolution fusion | flops 1879048192 | bytes 10223616 | tf_op jit(solution)/shard_map/dot_general | solution.py:38
  217.6 9.6 %multiply_convert_fusion.5 = (bf16[1024,1792]{1,0:T(8,128)(2,1)S(1)}, bf16[1024,1792]{1,0:T(8,128)(2,1)}, bf16[1024,1792]{1,0:T(8,128)(2,1)}) fusion(f32[1024,1792]{1,0:T(8,128)} %fusion.20, f32[1024,1792]{1,0:T(8,128)S(1)} %fusion.9, bf16[1024,512]{1,0:T(8,128)(2,1)S(1)} %bitcast.142, bf16[1,2,1792,512]{3,2,1,0:T(8,128)(2,1)S(1)} %bitcast.132), kind=kOutput, calls=%fused_computation.12 | convolution fusion | flops 1906573312 | bytes 28573696 | tf_op jit(solution)/shard_map/dot_general | solution.py:38
  227.2 5.5 %fusion.4 = bf16[1792,1,512]{2,0,1:T(8,128)(2,1)S(1)} fusion(bf16[1024,1792]{1,0:T(8,128)(2,1)} %get-tuple-element.19, bf16[1024,512]{1,0:T(8,128)(2,1)S(1)} %multiply_convert_fusion.7), kind=kOutput, calls=%fused_computation.27 | convolution fusion | flops 1879965696 | bytes 6553600 | tf_op jit(solution)/shard_map/rf,rd->fd/dot_general | solution.py:73
  232.7 2.1 fusion.3
  234.9 2.1 fusion.2
  237.0 2.9 pad_maximum_fusion
  242.9 3.1 copy.55
  248.2 5.7 %multiply_reduce_fusion = bf16[1024]{0:T(1024)(128)(2,1)S(1)} fusion(f32[1024,512]{0,1:T(8,128)} %copy.55, bf16[1024,1792]{1,0:T(8,128)(2,1)} %get-tuple-element.22, bf16[1792,1536]{1,0:T(8,128)(2,1)} %all-gather.5.cloned.1.call-done), kind=kOutput, calls=%fused_computation.33 | convolution fusion | flops 1880095744 | bytes 7604224 | tf_op jit(solution)/shard_map/dot_general | solution.py:49
  253.9 4.7 %multiply_reduce_fusion.1 = bf16[1024]{0:T(1024)(128)(2,1)S(1)} fusion(f32[1024,512]{0,1:T(8,128)S(1)} %copy-done.10, bf16[1024,1792]{1,0:T(8,128)(2,1)} %get-tuple-element.19, bf16[1792,1536]{1,0:T(8,128)(2,1)} %all-gather.3.cloned.1.call-done), kind=kOutput, calls=%fused_computation.34 | convolution fusion | flops 1880095744 | bytes 7604224 | tf_op jit(solution)/shard_map/dot_general | solution.py:49
  259.1 4.8 %fusion.12 = f32[1024,512]{1,0:T(8,128)S(1)} fusion(bf16[1024,1792]{1,0:T(8,128)(2,1)} %get-tuple-element.23, bf16[1,2,1792,512]{3,2,1,0:T(8,128)(2,1)} %bitcast.129), kind=kOutput, calls=%fused_computation.47 | convolution fusion | flops 1879048192 | bytes 7602176 | tf_op jit(solution)/shard_map/dot_general | solution.py:61
  264.0 2.0 fusion.8
  267.1 2.0 add_convert_fusion
  269.2 2.1 add_convert_fusion.1
  271.2 1.9 pad_maximum_fusion.3
  273.1 5.2 %all-to-all-start.2 = ((bf16[2,16,64,513]{3,2,0,1:T(8,128)(2,1)}), bf16[2,16,64,513]{3,2,0,1:T(8,128)(2,1)S(1)}, u32[]{:S(2)}, u32[]{:S(2)}) async-start(bf16[2,16,64,513]{3,2,0,1:T(8,128)(2,1)} %pad_maximum_fusion.3), calls=%async_computation.2 | async-start | bytes 5242880 | tf_op jit(solution)/shard_map/all_to_all | solution.py:16
  278.3 39.6 %all-to-all-done.2 = bf16[2,16,64,513]{3,2,0,1:T(8,128)(2,1)S(1)} async-done(((bf16[2,16,64,513]{3,2,0,1:T(8,128)(2,1)}), bf16[2,16,64,513]{3,2,0,1:T(8,128)(2,1)S(1)}, u32[]{:S(2)}, u32[]{:S(2)}) %all-to-all-start.2) | async-done | bytes 2101280 | tf_op jit(solution)/shard_map/all_to_all | solution.py:16
  319.8 9.2 %gather_fusion = bf16[2048,512]{1,0:T(8,128)(2,1)} fusion(bf16[2048,512]{1,0:T(8,128)(2,1)S(1)} %bitcast.124, s32[2048]{0:T(1024)S(1)} %broadcast_clamp_fusion), kind=kCustom, calls=%fused_computation | custom fusion | bytes 4202496 | tf_op jit(solution)/shard_map/gather | solution.py:145
  329.0 2.8 reshape.277
  331.8 6.7 %reduce_sum.32 = bf16[1024,512]{1,0:T(8,128)(2,1)} reduce(bf16[1024,2,512]{2,1,0:T(2,128)(2,1)S(1)} %reshape.277, bf16[]{:T(256)} %constant.31.clone.1), dimensions={1}, to_apply=%region_5.6 | reduce | flops 524288 | bytes 3145730 | tf_op jit(solution)/shard_map/reduce_sum | solution.py:147
  338.5 2.3 reshape.278
  341.2 13.1 %gather_fusion.1 = bf16[2048]{0:T(1024)(128)(2,1)S(1)} fusion(bf16[2048]{0:T(1024)(128)(2,1)S(1)} %reshape_reshape.8, s32[2048]{0:T(1024)S(1)} %broadcast_clamp_fusion), kind=kCustom, calls=%fused_computation.1 | custom fusion | bytes 16384 | tf_op jit(solution)/shard_map/gather | solution.py:149
  356.6 34.6 %reduce-scatter.3.cloned.1.call-done = bf16[224,3,512]{2,0,1:T(8,128)(2,1)} async-done(((bf16[1792,3,512]{2,0,1:T(8,128)(2,1)}), bf16[224,3,512]{2,0,1:T(8,128)(2,1)}) %reduce-scatter.3.cloned.1.call-update) | async-done | bytes 688144 | tf_op jit(solution)/shard_map/reduce_scatter | solution.py:69
  (108 shorter events, 37.3 us)
Async XLA Ops:
  7.2 118.8 %all-gather.5.cloned.1.call-start = ((), (), s32[]{:S(2)}) async-start(), calls=%async_computation.6 | async-start | bytes 6193152 | tf_op jit(solution)/shard_map/all_gather | solution.py:27
  10.0 2.5 copy-start.14
  10.1 3.0 copy-start.15
  11.0 2.8 copy-start.11
  11.0 183.6 %all-gather.3.cloned.1.call-start = ((), (), s32[]{:S(2)}) async-start(), calls=%async_computation.5 | async-start | bytes 6193152 | tf_op jit(solution)/shard_map/all_gather | solution.py:27
  28.3 8.3 %copy-start.16 = (bf16[128,8,2]{0,2,1:T(2,128)(2,1)S(1)}, bf16[128,8,2]{0,2,1:T(2,128)(2,1)}, u32[]{:S(2)}) copy-start(bf16[128,8,2]{0,2,1:T(2,128)(2,1)} %param.11) | copy-start | bytes 12292
  29.8 47.2 %all-to-all-start.1 = ((bf16[2,16,64,512]{3,2,0,1:T(8,128)(2,1)}), bf16[2,16,64,512]{3,2,0,1:T(8,128)(2,1)S(1)}, u32[]{:S(2)}, u32[]{:S(2)}) async-start(bf16[2,16,64,512]{3,2,0,1:T(8,128)(2,1)} %copy.47), calls=%async_computation.1 | async-start | bytes 4194304 | tf_op jit(solution)/shard_map/all_to_all | solution.py:116
  57.5 15.7 %copy-start.9 = (bf16[2,16,64,1]{3,2,1,0:T(8,128)(2,1)S(1)}, bf16[2,16,64,1]{3,2,1,0:T(8,128)(2,1)}, u32[]{:S(2)}) copy-start(bf16[2,16,64,1]{3,2,1,0:T(8,128)(2,1)} %reshape_reshape.9) | copy-start | bytes 12292
  77.0 1.4 copy-start.4
  78.3 44.7 %all-to-all-start = ((bf16[2,16,64,513]{3,2,0,1:T(8,128)(2,1)}), bf16[2,16,64,513]{3,2,0,1:T(8,128)(2,1)S(1)}, u32[]{:S(2)}, u32[]{:S(2)}) async-start(bf16[2,16,64,513]{3,2,0,1:T(8,128)(2,1)} %copy.44), calls=%async_computation | async-start | bytes 5242880 | tf_op jit(solution)/shard_map/all_to_all | solution.py:16
  84.1 271.5 %reduce-scatter.5.cloned.1.call-start = ((), (), s32[]{:S(2)}) async-start(), calls=%async_computation.8 | async-start | bytes 6193152 | tf_op jit(solution)/shard_map/reduce_scatter | solution.py:69
  124.6 1.0 copy-start.2
  137.8 2.8 copy-start.13
  140.5 8.8 %copy-start.5 = (bf16[1792,1,2,512]{3,0,2,1:T(8,128)(2,1)}, bf16[1792,1,2,512]{3,0,2,1:T(8,128)(2,1)S(1)}, u32[]{:S(2)}) copy-start(bf16[1792,1,2,512]{3,0,2,1:T(8,128)(2,1)S(1)} %copy.66) | copy-start | bytes 11010052
  158.7 7.7 %copy-start.17 = (bf16[1024,1792]{1,0:T(8,128)(2,1)}, bf16[1024,1792]{1,0:T(8,128)(2,1)S(1)}, u32[]{:S(2)}) copy-start(bf16[1024,1792]{1,0:T(8,128)(2,1)S(1)} %get-tuple-element.21) | copy-start | bytes 11010052
  158.7 5.5 %copy-start.21 = (bf16[1024,1792]{1,0:T(8,128)(2,1)S(1)}, bf16[1024,1792]{1,0:T(8,128)(2,1)}, u32[]{:S(2)}) copy-start(bf16[1024,1792]{1,0:T(8,128)(2,1)} %get-tuple-element.23) | copy-start | bytes 11010052
  171.5 1.2 copy-start.1
  171.6 219.6 %reduce-scatter.3.cloned.1.call-start = ((), (), s32[]{:S(2)}) async-start(), calls=%async_computation.7 | async-start | bytes 6193152 | tf_op jit(solution)/shard_map/reduce_scatter | solution.py:69
  206.2 2.7 copy-start.12
  208.9 8.7 %copy-start.7 = (bf16[1792,1,2,512]{3,0,2,1:T(8,128)(2,1)}, bf16[1792,1,2,512]{3,0,2,1:T(8,128)(2,1)S(1)}, u32[]{:S(2)}) copy-start(bf16[1792,1,2,512]{3,0,2,1:T(8,128)(2,1)S(1)} %copy.67) | copy-start | bytes 11010052
  227.2 7.7 %copy-start.19 = (bf16[1024,1792]{1,0:T(8,128)(2,1)}, bf16[1024,1792]{1,0:T(8,128)(2,1)S(1)}, u32[]{:S(2)}) copy-start(bf16[1024,1792]{1,0:T(8,128)(2,1)S(1)} %get-tuple-element.18) | copy-start | bytes 11010052
  227.2 5.5 %copy-start.22 = (bf16[1024,1792]{1,0:T(8,128)(2,1)S(1)}, bf16[1024,1792]{1,0:T(8,128)(2,1)}, u32[]{:S(2)}) copy-start(bf16[1024,1792]{1,0:T(8,128)(2,1)} %get-tuple-element.20) | copy-start | bytes 11010052
  239.9 1.3 copy-start.3
  248.2 5.7 %copy-start.10 = (f32[1024,512]{0,1:T(8,128)S(1)}, f32[1024,512]{0,1:T(8,128)}, u32[]{:S(2)}) copy-start(f32[1024,512]{0,1:T(8,128)} %copy.54) | copy-start | bytes 6291460
  259.1 4.8 %copy-start.8 = (bf16[1792,1,2,512]{3,0,2,1:T(8,128)(2,1)S(1)}, bf16[1792,1,2,512]{3,0,2,1:T(8,128)(2,1)}, u32[]{:S(2)}) copy-start(bf16[1792,1,2,512]{3,0,2,1:T(8,128)(2,1)} %copy-done.7) | copy-start | bytes 11010052
  259.1 4.8 %copy-start.23 = (bf16[1024,1792]{1,0:T(8,128)(2,1)S(1)}, bf16[1024,1792]{1,0:T(8,128)(2,1)}, u32[]{:S(2)}) copy-start(bf16[1024,1792]{1,0:T(8,128)(2,1)} %get-tuple-element.20) | copy-start | bytes 11010052
  263.9 2.1 copy-start.6
  264.0 3.2 copy-start.18
  267.1 2.1 copy-start.20
  273.1 44.8 %all-to-all-start.2 = ((bf16[2,16,64,513]{3,2,0,1:T(8,128)(2,1)}), bf16[2,16,64,513]{3,2,0,1:T(8,128)(2,1)S(1)}, u32[]{:S(2)}, u32[]{:S(2)}) async-start(bf16[2,16,64,513]{3,2,0,1:T(8,128)(2,1)} %pad_maximum_fusion.3), calls=%async_computation.2 | async-start | bytes 5242880 | tf_op jit(solution)/shard_map/all_to_all | solution.py:16
  317.9 1.5 copy-start
  331.8 9.0 %slice-start = ((bf16[2,16,64,513]{3,2,0,1:T(8,128)(2,1)}), bf16[2,16,64,1]{3,2,0,1:T(8,128)(2,1)S(1)}, s32[]{:S(2)}) async-start(bf16[2,16,64,513]{3,2,0,1:T(8,128)(2,1)} %copy-done), calls=%async_computation.9 | async-start | bytes 1048576 | tf_op jit(solution)/shard_map/split | solution.py:17
Sparse Core Ops, SparseCore 0:
  11.1 101.8 all-gather.4
  115.4 79.2 all-gather.2
  198.6 91.2 reduce-scatter.4
  293.7 97.4 reduce-scatter.2
where the time goes:
time: 410 us; the launch traced here: 403 us
  local copies, waits for them, and re-layouts  138 us (34%)
  waiting for transfers between devices  132 us (32%)
  matrix products  77.4 us (19%)
  other arithmetic  23.1 us (6%)
  starting transfers between devices  17.9 us (4%)
  between operations  14.7 us (4%)
    all_to_all x2, waiting for transfers between devices, side_by_side(): lax.all_to_all(both, axis, split_axis=split_dim, concat_axis=concat_dim,...  75.3 us
    dot_general x6, matrix products, contract_last(): lax.dot_general(former, latter, (((1,), (1,)), ((), ())), preferred_eleme...  36.4 us
    reduce_scatter x2, waiting for transfers between devices, reduce_grads(): lax.psum_scatter(jnp.concatenate([jnp.stack([gate_term, up_term], axis=1)...  34.6 us
    scatter x2, local copies, waits for them, and re-layouts, spread(): jnp.zeros((buffer_rows, DS), jnp.bfloat16).at[flat_place].set(doubled)  22.1 us
    all_gather x2, waiting for transfers between devices, rows_first(): filled = lax.all_gather(both, axis, axis=0, tiled=True)  21.6 us
    reshape x4, local copies, waits for them, and re-layouts, rows_first(): b.reshape(-1, *t.shape[1:])  20.4 us
    scatter x1, local copies, waits for them, and re-layouts, body(): jnp.zeros((buffer_rows,), jnp.bfloat16).at[flat_place]  14.6 us
    gather x1, local copies, waits for them, and re-layouts, body(): returned_router.reshape(buffer_rows)[flat_place].reshape(token_count, H, 2)  13.1 us
  transfers between devices with their start and end apart: 7, of which 4 were waited for; matrix products, arithmetic and copies ran while one was open for 55% of the time, Pallas kernels for 0%

commit v1 on v0

--- a/solution.py
+++ b/solution.py
@@ -24,7 +24,17 @@
     turned = [jnp.moveaxis(a, dim, 0) for a, dim in zip(arrays, dims)]
     widths = [t[0].size for t in turned]
     both = jnp.concatenate([t.reshape(-1, w) for t, w in zip(turned, widths)], axis=1)
-    filled = lax.all_gather(both, axis, axis=0, tiled=True)
+
+    def proceed_the_rings(chunk, across, ndim_at):
+        block_now = lax.all_to_all(
+            jnp.stack([chunk] * lax.psum(1, axis_name=across), axis=0),
+            axis_name=across,
+            split_axis=0,
+            concat_axis=0,
+        )
+        return jnp.concatenate(block_now, axis=ndim_at)
+
+    filled = proceed_the_rings(both, axis, 0)
     tiles = jnp.split(filled, [sum(widths[:k]) for k in range(1, len(widths))], axis=1)
     return tuple(
         (

time: 410 us -> 535 us (1.30)
  waiting for transfers between devices: 132 us -> 247 us
  starting transfers between devices: 17.9 us -> 28 us
    all_to_all x0 -> x2, waiting for transfers between devices: none -> 164 us  [proceed_the_rings(): lax.all_to_all(jnp.stack([chunk] * lax.psum(1, axis_name=across), axis=0)...]
    reduce_scatter x2, waiting for transfers between devices: 34.6 us -> 0.02 us  [reduce_grads(): lax.psum_scatter(jnp.concatenate([jnp.stack([gate_term, up_term], axis=1)...]
    all_gather x2 -> x0, waiting for transfers between devices: 21.6 us -> none  [rows_first(): filled = lax.all_gather(both, axis, axis=0, tiled=True)]
    reshape x4 -> x0, local copies, waits for them, and re-layouts: 20.4 us -> none  [rows_first(): b.reshape(-1, *t.shape[1:])]
    split x2 -> x4, local copies, waits for them, and re-layouts: 8.39 us -> 21.1 us  [rows_first(): jnp.split(filled, [sum(widths[:k]) for k in range(1, len(widths))], axis=1)]
    all_to_all x0 -> x2, starting transfers between devices: none -> 11.7 us  [proceed_the_rings(): lax.all_to_all(jnp.stack([chunk] * lax.psum(1, axis_name=across), axis=0)...]
    all_to_all x2, waiting for transfers between devices: 75.3 us -> 82.8 us  [side_by_side(): lax.all_to_all(both, axis, split_axis=split_dim, concat_axis=concat_dim,...]
    another operation x0 -> x2, local copies, waits for them, and re-layouts: none -> 5.68 us  [proceed_the_rings(): jnp.stack([chunk] * lax.psum(1, axis_name=across), axis=0)]
  transfers between devices with their start and end apart: 7 -> 7, of which waited for: 4 -> 4; matrix products, arithmetic and copies ran while one was open for 55% -> 30% of each run, Pallas kernels for 0% -> 0%
where the time goes in v1:
time: 535 us; the launch traced here: 526 us
  waiting for transfers between devices  247 us (46%)
  local copies, waits for them, and re-layouts  138 us (26%)
  matrix products  77.9 us (15%)
  starting transfers between devices  28 us (5%)
  other arithmetic  20.4 us (4%)
  between operations  15 us (3%)
    all_to_all x2, waiting for transfers between devices, proceed_the_rings(): lax.all_to_all(jnp.stack([chunk] * lax.psum(1, axis_name=across), axis=0)...  164 us
    all_to_all x2, waiting for transfers between devices, side_by_side(): lax.all_to_all(both, axis, split_axis=split_dim, concat_axis=concat_dim,...  82.8 us
    dot_general x6, matrix products, contract_last(): lax.dot_general(former, latter, (((1,), (1,)), ((), ())), preferred_eleme...  36.6 us
    scatter x2, local copies, waits for them, and re-layouts, spread(): jnp.zeros((buffer_rows, DS), jnp.bfloat16).at[flat_place].set(doubled)  22.1 us
    split x4, local copies, waits for them, and re-layouts, rows_first(): jnp.split(filled, [sum(widths[:k]) for k in range(1, len(widths))], axis=1)  21.1 us
    scatter x1, local copies, waits for them, and re-layouts, body(): jnp.zeros((buffer_rows,), jnp.bfloat16).at[flat_place]  14.8 us
    gather x1, local copies, waits for them, and re-layouts, body(): returned_router.reshape(buffer_rows)[flat_place].reshape(token_count, H, 2)  13.1 us
    all_to_all x2, starting transfers between devices, proceed_the_rings(): lax.all_to_all(jnp.stack([chunk] * lax.psum(1, axis_name=across), axis=0)...  11.7 us
  transfers between devices with their start and end apart: 7, of which 4 were waited for; matrix products, arithmetic and copies ran while one was open for 30% of the time, Pallas kernels for 0%

profile of v1, /device:TPU:0, one launch (start us, length us, event | category | flops | bytes accessed | tf_op | source)
XLA Modules:
  0.0 525.6 jit_solution(11343858517513910182)
XLA Ops:
  12.3 2.2 reshape.332
  14.7 10.6 %scatter_custom_fusion.2 = bf16[2048,512]{1,0:T(8,128)(2,1)S(1)} fusion(s32[2048]{0:T(1024)S(1)} %bitcast.162, bf16[2048,512]{1,0:T(8,128)(2,1)} %reshape.332, bf16[]{:T(256)} %constant.31.clone.1), kind=kCustom, calls=%fused_computation.57 | custom fusion | bytes 2097664 | tf_op jit(solution)/shard_map/scatter | solution.py:117
  26.8 6.5 %all-to-all-start.2 = ((bf16[2,16,64,512]{3,2,0,1:T(8,128)(2,1)}), bf16[2,16,64,512]{3,2,0,1:T(8,128)(2,1)S(1)}, u32[]{:S(2)}, u32[]{:S(2)}) async-start(bf16[2,16,64,512]{3,2,0,1:T(8,128)(2,1)} %copy.68), calls=%async_computation.2 | async-start | bytes 4194304 | tf_op jit(solution)/shard_map/all_to_all | solution.py:126
  33.9 14.8 %scatter_custom_fusion.1 = bf16[2048]{0:T(1024)(128)(2,1)S(1)} fusion(s32[2048]{0:T(1024)S(1)} %bitcast.163, bf16[2048]{0:T(1024)(128)(2,1)S(1)} %reshape.324, bf16[]{:T(256)} %constant.31.clone.1), kind=kCustom, calls=%fused_computation.86 | custom fusion | bytes 4098 | tf_op jit(solution)/shard_map/scatter | solution.py:123
  52.0 2.4 broadcast_in_dim.33
  54.5 4.2 reshape.316
  58.6 11.5 %scatter_custom_fusion = bf16[2048,512]{1,0:T(8,128)(2,1)} fusion(s32[2048]{0:T(1024)S(1)} %bitcast.164, bf16[2048,512]{1,0:T(8,128)(2,1)} %reshape.316, bf16[]{:T(256)} %constant.31.clone.1), kind=kCustom, calls=%fused_computation.59 | custom fusion | bytes 2097664 | tf_op jit(solution)/shard_map/scatter | solution.py:117
  75.2 5.7 %all-to-all-start = ((bf16[2,16,64,513]{3,2,0,1:T(8,128)(2,1)}), bf16[2,16,64,513]{3,2,0,1:T(8,128)(2,1)S(1)}, u32[]{:S(2)}, u32[]{:S(2)}) async-start(bf16[2,16,64,513]{3,2,0,1:T(8,128)(2,1)} %copy.65), calls=%async_computation | async-start | bytes 5242880 | tf_op jit(solution)/shard_map/all_to_all | solution.py:16
  82.5 31.9 %all-to-all-done = bf16[2,16,64,513]{3,2,0,1:T(8,128)(2,1)S(1)} async-done(((bf16[2,16,64,513]{3,2,0,1:T(8,128)(2,1)}), bf16[2,16,64,513]{3,2,0,1:T(8,128)(2,1)S(1)}, u32[]{:S(2)}, u32[]{:S(2)}) %all-to-all-start) | async-done | bytes 2101280 | tf_op jit(solution)/shard_map/all_to_all | solution.py:16
  114.4 2.8 stack.32
  117.2 6.6 %all-to-all-start.1 = ((bf16[8,224,1536]{2,1,0:T(8,128)(2,1)}), bf16[8,224,1536]{2,1,0:T(8,128)(2,1)}, u32[]{:S(2)}, u32[]{:S(2)}) async-start(bf16[8,224,1536]{2,1,0:T(8,128)(2,1)} %stack.32), calls=%async_computation.1 | async-start | bytes 11010048 | tf_op jit(solution)/shard_map/all_to_all | solution.py:29
  123.9 3.1 fusion.32
  129.9 70.8 %all-to-all-done.1 = bf16[8,224,1536]{2,1,0:T(8,128)(2,1)} async-done(((bf16[8,224,1536]{2,1,0:T(8,128)(2,1)}), bf16[8,224,1536]{2,1,0:T(8,128)(2,1)}, u32[]{:S(2)}, u32[]{:S(2)}) %all-to-all-start.1) | async-done | bytes 5505056 | tf_op jit(solution)/shard_map/all_to_all | solution.py:29
  200.7 4.2 split.27
  204.9 6.3 %copy.69 = bf16[1792,1024]{0,1:T(8,128)(2,1)} copy(bf16[1792,1024]{1,0:T(8,128)(2,1)} %split.27) | data formatting | bytes 7340032 | tf_op jit(solution)/shard_map/split | solution.py:38
  211.3 3.7 fusion.20
  215.1 5.0 fusion.9
  220.0 9.5 %multiply_convert_fusion.5 = (bf16[1024,1792]{1,0:T(8,128)(2,1)}, bf16[1024,1792]{1,0:T(8,128)(2,1)}, bf16[1024,1792]{1,0:T(8,128)(2,1)S(1)}) fusion(f32[1024,1792]{1,0:T(8,128)S(1)} %fusion.20, f32[1024,1792]{1,0:T(8,128)} %fusion.9, bf16[1024,512]{1,0:T(8,128)(2,1)S(1)} %bitcast.159, bf16[1,2,1792,512]{2,3,1,0:T(8,128)(2,1)S(1)} %bitcast.142), kind=kOutput, calls=%fused_computation.12 | convolution fusion | flops 1906573312 | bytes 28573696 | tf_op jit(solution)/shard_map/dot_general | solution.py:48
  229.6 5.5 %fusion.4 = bf16[1792,1,512]{2,0,1:T(8,128)(2,1)S(1)} fusion(bf16[1024,1792]{1,0:T(8,128)(2,1)} %get-tuple-element.23, bf16[1024,512]{1,0:T(8,128)(2,1)S(1)} %multiply_convert_fusion.7), kind=kOutput, calls=%fused_computation.25 | convolution fusion | flops 1879965696 | bytes 6553600 | tf_op jit(solution)/shard_map/rf,rd->fd/dot_general | solution.py:83
  235.1 2.1 fusion.2
  237.3 2.1 fusion.3
  239.4 2.9 pad_maximum_fusion
  244.0 2.9 stack.68
  246.8 5.1 all-to-all-start.3
  252.3 93.0 %all-to-all-done.3 = bf16[8,224,1536]{2,1,0:T(8,128)(2,1)} async-done(((bf16[8,224,1536]{2,1,0:T(8,128)(2,1)}), bf16[8,224,1536]{2,1,0:T(8,128)(2,1)}, u32[]{:S(2)}, u32[]{:S(2)}) %all-to-all-start.3) | async-done | bytes 5505056 | tf_op jit(solution)/shard_map/all_to_all | solution.py:29
  345.3 4.4 split.29
  349.6 6.1 %copy.74 = bf16[1792,1024]{0,1:T(8,128)(2,1)} copy(bf16[1792,1024]{1,0:T(8,128)(2,1)} %split.29) | data formatting | bytes 7340032 | tf_op jit(solution)/shard_map/split | solution.py:38
  355.8 3.7 fusion.17
  359.6 5.0 fusion.13
  364.5 9.6 %multiply_convert_fusion.3 = (bf16[1024,1792]{1,0:T(8,128)(2,1)}, bf16[1024,1792]{1,0:T(8,128)(2,1)}, bf16[1024,1792]{1,0:T(8,128)(2,1)S(1)}) fusion(f32[1024,1792]{1,0:T(8,128)S(1)} %fusion.17, f32[1024,1792]{1,0:T(8,128)} %fusion.13, bf16[1024,512]{1,0:T(8,128)(2,1)S(1)} %bitcast.155, bf16[1,2,1792,512]{2,3,1,0:T(8,128)(2,1)S(1)} %bitcast.145), kind=kOutput, calls=%fused_computation.8 | convolution fusion | flops 1906573312 | bytes 28573696 | tf_op jit(solution)/shard_map/dot_general | solution.py:48
  374.1 5.5 %fusion.7 = bf16[1792,1,512]{2,0,1:T(8,128)(2,1)S(1)} fusion(bf16[1024,1792]{1,0:T(8,128)(2,1)} %get-tuple-element.26, bf16[1024,512]{1,0:T(8,128)(2,1)S(1)} %multiply_convert_fusion.6), kind=kOutput, calls=%fused_computation.28 | convolution fusion | flops 1879965696 | bytes 6553600 | tf_op jit(solution)/shard_map/rf,rd->fd/dot_general | solution.py:83
  379.7 2.1 fusion.5
  381.8 2.1 fusion.6
  383.9 3.0 pad_maximum_fusion.1
  389.8 2.9 copy.79
  393.0 2.0 copy.80
  395.1 5.5 %multiply_reduce_fusion.1 = bf16[1024]{0:T(1024)(128)(2,1)S(1)} fusion(f32[1024,512]{0,1:T(8,128)} %copy.79, bf16[1024,1792]{1,0:T(8,128)(2,1)} %get-tuple-element.23, bf16[1792,1536]{1,0:T(8,128)(2,1)} %bitcast.5), kind=kOutput, calls=%fused_computation.32 | convolution fusion | flops 1880095744 | bytes 7604224 | tf_op jit(solution)/shard_map/dot_general | solution.py:59
  400.6 4.7 multiply_reduce_fusion
  405.8 5.3 %fusion.8 = f32[1024,512]{1,0:T(8,128)S(1)} fusion(bf16[1024,1792]{1,0:T(8,128)(2,1)} %copy-done.17, bf16[1,2,1792,512]{2,3,1,0:T(8,128)(2,1)} %bitcast.140), kind=kOutput, calls=%fused_computation.41 | convolution fusion | flops 1879048192 | bytes 7602176 | tf_op jit(solution)/shard_map/dot_general | solution.py:71
  411.2 2.1 fusion.12
  414.3 2.1 add_convert_fusion.1
  416.4 2.1 add_convert_fusion
  420.5 4.0 all-to-all-start.4
  424.5 50.9 %all-to-all-done.4 = bf16[2,16,64,513]{3,2,0,1:T(8,128)(2,1)S(1)} async-done(((bf16[2,16,64,513]{3,2,0,1:T(8,128)(2,1)}), bf16[2,16,64,513]{3,2,0,1:T(8,128)(2,1)S(1)}, u32[]{:S(2)}, u32[]{:S(2)}) %all-to-all-start.4) | async-done | bytes 2101280 | tf_op jit(solution)/shard_map/all_to_all | solution.py:16
  479.2 13.1 %gather_fusion.1 = bf16[2048]{0:T(1024)(128)(2,1)S(1)} fusion(bf16[2048]{0:T(1024)(128)(2,1)S(1)} %reshape_reshape.8, s32[2048]{0:T(1024)S(1)} %broadcast_clamp_fusion), kind=kCustom, calls=%fused_computation.1 | custom fusion | bytes 16384 | tf_op jit(solution)/shard_map/gather | solution.py:159
  492.3 9.2 %gather_fusion = bf16[2048,512]{1,0:T(8,128)(2,1)} fusion(bf16[2048,512]{1,0:T(8,128)(2,1)S(1)} %bitcast.137, s32[2048]{0:T(1024)S(1)} %broadcast_clamp_fusion), kind=kCustom, calls=%fused_computation | custom fusion | bytes 4202496 | tf_op jit(solution)/shard_map/gather | solution.py:155
  501.5 2.7 reshape.289
  504.3 5.6 %reduce_sum.32 = bf16[1024,512]{1,0:T(8,128)(2,1)S(1)} reduce(bf16[1024,2,512]{2,1,0:T(2,128)(2,1)S(1)} %reshape.289, bf16[]{:T(256)} %constant.31.clone.1), dimensions={1}, to_apply=%region_5.6 | reduce | flops 524288 | bytes 3145730 | tf_op jit(solution)/shard_map/reduce_sum | solution.py:157
  (106 shorter events, 41.1 us)
Async XLA Ops:
  25.3 8.1 %copy-start.16 = (bf16[128,8,2]{0,2,1:T(2,128)(2,1)S(1)}, bf16[128,8,2]{0,2,1:T(2,128)(2,1)}, u32[]{:S(2)}) copy-start(bf16[128,8,2]{0,2,1:T(2,128)(2,1)} %param.11) | copy-start | bytes 12292
  26.8 47.1 %all-to-all-start.2 = ((bf16[2,16,64,512]{3,2,0,1:T(8,128)(2,1)}), bf16[2,16,64,512]{3,2,0,1:T(8,128)(2,1)S(1)}, u32[]{:S(2)}, u32[]{:S(2)}) async-start(bf16[2,16,64,512]{3,2,0,1:T(8,128)(2,1)} %copy.68), calls=%async_computation.2 | async-start | bytes 4194304 | tf_op jit(solution)/shard_map/all_to_all | solution.py:126
  54.5 15.7 %copy-start.9 = (bf16[2,16,64,1]{3,2,1,0:T(8,128)(2,1)S(1)}, bf16[2,16,64,1]{3,2,1,0:T(8,128)(2,1)}, u32[]{:S(2)}) copy-start(bf16[2,16,64,1]{3,2,1,0:T(8,128)(2,1)} %reshape_reshape.9) | copy-start | bytes 12292
  73.9 7.1 %copy-start.14 = (bf16[2,2,224,512]{3,2,1,0:T(8,128)(2,1)S(1)}, bf16[2,2,224,512]{3,2,1,0:T(8,128)(2,1)}, u32[]{:S(2)}) copy-start(bf16[2,2,224,512]{3,2,1,0:T(8,128)(2,1)} %param.12) | copy-start | bytes 2752516
  73.9 1.4 copy-start.4
  75.2 39.1 %all-to-all-start = ((bf16[2,16,64,513]{3,2,0,1:T(8,128)(2,1)}), bf16[2,16,64,513]{3,2,0,1:T(8,128)(2,1)S(1)}, u32[]{:S(2)}, u32[]{:S(2)}) async-start(bf16[2,16,64,513]{3,2,0,1:T(8,128)(2,1)} %copy.65), calls=%async_computation | async-start | bytes 5242880 | tf_op jit(solution)/shard_map/all_to_all | solution.py:16
  81.0 1.4 copy-start.15
  117.2 83.5 %all-to-all-start.1 = ((bf16[8,224,1536]{2,1,0:T(8,128)(2,1)}), bf16[8,224,1536]{2,1,0:T(8,128)(2,1)}, u32[]{:S(2)}, u32[]{:S(2)}) async-start(bf16[8,224,1536]{2,1,0:T(8,128)(2,1)} %stack.32), calls=%async_computation.1 | async-start | bytes 11010048 | tf_op jit(solution)/shard_map/all_to_all | solution.py:29
  123.8 388.6 %reduce-scatter.3.cloned.1.call-start = ((), (), s32[]{:S(2)}) async-start(), calls=%async_computation.7 | async-start | bytes 6193152 | tf_op jit(solution)/shard_map/reduce_scatter | solution.py:79
  128.6 1.0 copy-start.2
  211.3 3.8 copy-start.5
  211.3 3.8 copy-start.13
  229.6 7.7 %copy-start.17 = (bf16[1024,1792]{1,0:T(8,128)(2,1)}, bf16[1024,1792]{1,0:T(8,128)(2,1)S(1)}, u32[]{:S(2)}) copy-start(bf16[1024,1792]{1,0:T(8,128)(2,1)S(1)} %get-tuple-element.24) | copy-start | bytes 11010052
  229.6 5.5 %copy-start.20 = (bf16[1024,1792]{1,0:T(8,128)(2,1)S(1)}, bf16[1024,1792]{1,0:T(8,128)(2,1)}, u32[]{:S(2)}) copy-start(bf16[1024,1792]{1,0:T(8,128)(2,1)} %get-tuple-element.22) | copy-start | bytes 11010052
  242.3 1.0 copy-start.11
  246.8 5.2 copy-start.1
  246.8 98.5 %all-to-all-start.3 = ((bf16[8,224,1536]{2,1,0:T(8,128)(2,1)}), bf16[8,224,1536]{2,1,0:T(8,128)(2,1)}, u32[]{:S(2)}, u32[]{:S(2)}) async-start(bf16[8,224,1536]{2,1,0:T(8,128)(2,1)} %stack.68), calls=%async_computation.3 | async-start | bytes 11010048 | tf_op jit(solution)/shard_map/all_to_all | solution.py:29
  251.9 261.7 %reduce-scatter.5.cloned.1.call-start = ((), (), s32[]{:S(2)}) async-start(), calls=%async_computation.8 | async-start | bytes 6193152 | tf_op jit(solution)/shard_map/reduce_scatter | solution.py:79
  355.8 3.8 copy-start.7
  355.8 3.8 copy-start.12
  374.1 7.7 %copy-start.18 = (bf16[1024,1792]{1,0:T(8,128)(2,1)}, bf16[1024,1792]{1,0:T(8,128)(2,1)S(1)}, u32[]{:S(2)}) copy-start(bf16[1024,1792]{1,0:T(8,128)(2,1)S(1)} %get-tuple-element.27) | copy-start | bytes 11010052
  374.1 5.5 %copy-start.22 = (bf16[1024,1792]{1,0:T(8,128)(2,1)S(1)}, bf16[1024,1792]{1,0:T(8,128)(2,1)}, u32[]{:S(2)}) copy-start(bf16[1024,1792]{1,0:T(8,128)(2,1)} %get-tuple-element.25) | copy-start | bytes 11010052
  386.9 1.2 copy-start.3
  395.1 5.6 %copy-start.10 = (f32[1024,512]{0,1:T(8,128)S(1)}, f32[1024,512]{0,1:T(8,128)}, u32[]{:S(2)}) copy-start(f32[1024,512]{0,1:T(8,128)} %copy.80) | copy-start | bytes 6291460
  405.8 5.3 %copy-start.8 = (bf16[1792,1024]{0,1:T(8,128)(2,1)S(1)}, bf16[1792,1024]{0,1:T(8,128)(2,1)}, u32[]{:S(2)}) copy-start(bf16[1792,1024]{0,1:T(8,128)(2,1)} %copy.74) | copy-start | bytes 11010052
  405.8 5.3 %copy-start.19 = (bf16[1024,1792]{1,0:T(8,128)(2,1)S(1)}, bf16[1024,1792]{1,0:T(8,128)(2,1)}, u32[]{:S(2)}) copy-start(bf16[1024,1792]{1,0:T(8,128)(2,1)} %copy-done.18) | copy-start | bytes 11010052
  411.2 2.1 copy-start.6
  411.2 3.2 copy-start.21
  414.3 2.1 copy-start.23
  420.5 54.9 %all-to-all-start.4 = ((bf16[2,16,64,513]{3,2,0,1:T(8,128)(2,1)}), bf16[2,16,64,513]{3,2,0,1:T(8,128)(2,1)S(1)}, u32[]{:S(2)}, u32[]{:S(2)}) async-start(bf16[2,16,64,513]{3,2,0,1:T(8,128)(2,1)} %pad_maximum_fusion.3), calls=%async_computation.4 | async-start | bytes 5242880 | tf_op jit(solution)/shard_map/all_to_all | solution.py:16
  475.4 1.6 copy-start
  477.4 1.6 slice-start
Sparse Core Ops, SparseCore 0:
  242.5 152.2 reduce-scatter.2
  398.7 110.7 reduce-scatter.4
